TPU v7x, 32 devices: a whole 2x2x4 slice. The times are simulated.
32 devices in a mesh: lat: 8 (over z, y), ch: 4 (over x, core).
Axes of the slice: x: 2, y: 2, z: 4, core: 2. Of those that a mesh axis runs over, the one named last changes fastest.
Arguments:
- field: bfloat16 [728, 256, 1440], P('lat', 'ch'), may hold values from -6 to 6
- legendre: bfloat16 [384, 721, 728], P(('lat', 'ch')), may hold values from -0.21875 to 0.21875
- pair_order: int32 [384], replicated, may hold values from 0 to 383, each once
Outputs:
- coeffs: float32 [384, 721, 2, 256], P(('lat', 'ch'))
Inputs may be any that keep to these rules, and one draw needn't show every extreme that they name: `pair_order`: each of 0 to 383 appears once; a value p below 360 gives its bin the orders p and 719 - p, and a bin with a larger value is empty.
All inputs are finite; a program needn't handle non-finite values.
Results may differ from a plain program's by a relative error of at most 0.0037.
Values may be sent and summed in bfloat16 or wider, within the bound.
A program may use at most 256 MiB of HBM per device.

v0:
```python
import math
import jax
import jax.numpy as jnp
from jax import lax
from jax.sharding import PartitionSpec as P

NLAT = 721


def dft_table(points, modes, lon_count):
    turns = points[:, None] * modes[None, :] % lon_count
    angle = turns.astype(jnp.float32) * (2.0 * math.pi / lon_count)
    return jnp.stack([jnp.cos(angle), -jnp.sin(angle)], axis=-1).astype(jnp.bfloat16)


def project(basis_piece, data_rows, boundary, keep_mask):
    products = jnp.einsum(
        "brl,lbn->brn", basis_piece, data_rows, preferred_element_type=jnp.float32
    )
    bin_count, row_count, width_all = products.shape
    products = products.reshape(bin_count, row_count, 2, 2, width_all // 4)
    degree = jnp.arange(row_count, dtype=jnp.int32)
    upper_part = degree[None, :, None, None] < boundary[:, None, None, None]
    chosen = jnp.where(upper_part, products[:, :, 0], products[:, :, 1])
    return chosen * keep_mask[:, None, None, None].astype(jnp.float32)


def per_device(field, legendre, pair_order):
    lat_rows, chan_dev, lon_count = field.shape
    slot_count = pair_order.shape[0]
    lat_count = lax.axis_size("lat")
    group_size = slot_count // lat_count
    max_order = legendre.shape[1] - 1
    keep_all = pair_order < max_order // 2
    first_order = jnp.where(keep_all, pair_order, 0)
    orders = jnp.stack([first_order, max_order - 1 - first_order], axis=1)
    bound_all = max_order - first_order
    rows_global = lax.axis_index("lat") * lat_rows + jnp.arange(lat_rows, dtype=jnp.int32)
    masked = jnp.where((rows_global < NLAT)[:, None, None], field, jnp.zeros_like(field))
    norm_scale = 2.0 * math.pi / lon_count
    points = jnp.arange(lon_count, dtype=jnp.int32)
    dft_basis = dft_table(points, orders.reshape(-1), lon_count).reshape(lon_count, 4 * slot_count)
    fourier = jnp.einsum("ack,kn->anc", masked, dft_basis, preferred_element_type=jnp.float32)
    fourier = (fourier * norm_scale).astype(jnp.bfloat16).reshape(lat_rows, slot_count, 4, chan_dev)
    received = lax.all_to_all(
        fourier.reshape(lat_rows, slot_count, 4 * chan_dev),
        "lat",
        split_axis=1,
        concat_axis=0,
        tiled=True,
    )
    group_start = lax.axis_index("lat") * group_size
    bound_group = lax.dynamic_slice_in_dim(bound_all, group_start, group_size)
    keep_group = lax.dynamic_slice_in_dim(keep_all, group_start, group_size)
    part_sums = project(
        lax.all_gather(legendre, "ch", axis=0, tiled=True), received, bound_group, keep_group
    )
    return lax.all_to_all(part_sums, "ch", split_axis=0, concat_axis=3, tiled=True)


def solution(mesh):
    in_specs = (P("lat", "ch", None), P(("lat", "ch"), None, None), P())
    out_specs = P(("lat", "ch"), None, None, None)
    return jax.shard_map(
        per_device, mesh=mesh, in_specs=in_specs, out_specs=out_specs, check_vma=False
    )
```

profile of v0, /device:TPU:0, one launch (start us, length us, event | category | flops | bytes accessed | tf_op | source)
XLA Modules:
  0.0 950.9 jit_solution(16822089257262218695)
XLA Ops:
  6.5 0.0 all-gather.2.cloned.1.call-start
  6.5 0.7 all-gather.2.cloned.1.call-update
  7.3 0.7 broadcast_subtract_fusion.1
  8.0 0.1 copy.30
  8.1 0.1 mul.66
  8.3 19.0 %cosine_convert_fusion = (bf16[1440,768,1]{1,0,2:T(8,128)(2,1)S(1)}, bf16[1440,768,1]{1,0,2:T(8,128)(2,1)S(1)}) fusion(s32[768]{0:T(1024)S(1)} %mul.66), kind=kLoop, calls=%fused_computation.18 | loop fusion | flops 13271040 | bytes 4426752 | tf_op jit(solution)/shard_map/convert
  27.3 3.2 pad_maximum_fusion
  30.6 13.2 %copy.31 = bf16[1440,768,2]{0,2,1:T(2,128)(2,1)} copy(bf16[1440,768,2]{1,0,2:T(8,128)(2,1)} %pad_maximum_fusion) | data formatting | bytes 8847360 | tf_op jit(solution)/shard_map/stack | solution.py:13
  43.8 10.9 %convert_element_type.30 = bf16[1440,1536]{0,1:T(8,128)(2,1)} reshape(bf16[1440,768,2]{0,2,1:T(2,128)(2,1)} %copy.31) | data formatting | bytes 8847360 | tf_op jit(solution)/shard_map/convert_element_type | solution.py:13
  54.7 0.0 copy-start
  54.7 16.6 %broadcast_select_fusion = bf16[91,64,1440]{2,1,0:T(8,128)(2,1)} fusion(bf16[91,64,1440]{2,1,0:T(8,128)(2,1)} %param.3, pred[91]{0:T(512)(128)(4,1)S(1)} %add_compare_fusion), kind=kLoop, calls=%fused_computation.10 | loop fusion | flops 8386560 | bytes 33546332 | tf_op jit(solution)/shard_map/jit(_where)/select_n | solution.py:39
  71.3 0.0 copy-done
  71.3 49.8 %fusion = bf16[91,1536,64]{1,0,2:T(8,128)(2,1)} fusion(bf16[91,64,1440]{2,1,0:T(8,128)(2,1)} %broadcast_select_fusion, bf16[1440,1536]{0,1:T(8,128)(2,1)S(1)} %copy-done), kind=kOutput, calls=%fused_computation.1 | convolution fusion | flops 25781403648 | bytes 39088128 | tf_op jit(solution)/shard_map/ack,kn->anc/dot_general | solution.py:43
  121.2 31.3 %copy.34 = bf16[91,1536,64]{0,2,1:T(8,128)(2,1)} copy(bf16[91,1536,64]{1,0,2:T(8,128)(2,1)} %fusion) | data formatting | bytes 35782656 | tf_op jit(solution)/shard_map/convert_element_type | solution.py:44
  152.5 28.4 %copy.35 = bf16[91,384,256]{2,0,1:T(8,128)(2,1)} copy(bf16[91,384,256]{0,2,1:T(8,128)(2,1)} %bitcast.33) | data formatting | bytes 35782656 | tf_op jit(solution)/shard_map/reshape;reshape | solution.py:46
  180.9 0.0 copy-start.1
  180.9 7.3 all-to-all-start
  188.1 0.1 dynamic_slice.6
  188.2 0.0 copy-done.1
  188.2 0.1 dynamic-slice_convert_fusion
  188.3 0.1 iota_compare_fusion
  188.4 408.6 %all-to-all-done = bf16[91,384,256]{2,0,1:T(8,128)(2,1)} async-done(((bf16[91,384,256]{2,0,1:T(8,128)(2,1)}), bf16[91,384,256]{2,0,1:T(8,128)(2,1)}, u32[]{:S(2)}, u32[]{:S(2)}) %all-to-all-start) | async-done | bytes 17891360 | tf_op jit(solution)/shard_map/all_to_all | solution.py:45
  596.9 19.0 %copy.37 = bf16[8,91,48,256]{3,2,1,0:T(8,128)(2,1)} copy(bf16[8,91,48,256]{3,1,2,0:T(8,128)(2,1)} %bitcast.5) | data formatting | bytes 35782656 | tf_op jit(solution)/shard_map/all_to_all | solution.py:45
  615.9 0.0 all-gather.2.cloned.1.call-done
  615.9 36.0 %fusion.9 = f32[48,721,256]{2,1,0:T(8,128)} fusion(bf16[48,721,728]{2,1,0:T(8,128)(2,1)} %all-gather.2.cloned.1.call-done, bf16[728,48,256]{2,1,0:T(8,128)(2,1)} %bitcast.36), kind=kOutput, calls=%fused_computation.11 | convolution fusion | flops 12899647488 | bytes 103719168 | tf_op jit(solution)/shard_map/brl,lbn->brn/dot_general | solution.py:17
  651.9 36.0 %copy.39 = f32[48,721,256]{1,2,0:T(8,128)} copy(f32[48,721,256]{2,1,0:T(8,128)} %fusion.9) | data formatting | bytes 70877184 | tf_op jit(solution)/shard_map/brl,lbn->brn/dot_general | solution.py:17
  687.9 12.8 %fusion.2 = f32[48,721,2,64]{1,3,2,0:T(8,128)S(1)} fusion(f32[48,721,2,2,64]{1,4,3,2,0:T(8,128)} %bitcast.32, f32[48]{0:T(128)S(1)} %dynamic-slice_convert_fusion, pred[48,721]{1,0:T(8,128)(4,1)S(1)} %iota_compare_fusion), kind=kLoop, calls=%fused_computation.4 | loop fusion | flops 8859648 | bytes 53192688 | tf_op jit(solution)/shard_map/mul | solution.py:25
  700.8 208.6 %all_to_all.36 = f32[48,721,2,64]{1,3,2,0:T(8,128)S(1)} all-to-all(f32[48,721,2,64]{1,3,2,0:T(8,128)S(1)} %fusion.2), channel_id=1, replica_groups=mesh['lat'=8,'ch'=4] {'ch'}, dimensions={0} | all-to-all | bytes 35438592 | tf_op jit(solution)/shard_map/all_to_all | solution.py:58
  909.4 6.9 copy.41
  916.4 27.7 %copy.42 = f32[12,721,2,256]{3,2,1,0:T(2,128)} copy(f32[12,721,2,256]{1,3,2,0:T(8,128)} %bitcast.35) | data formatting | bytes 35438592 | tf_op jit(solution)/shard_map/all_to_all | solution.py:58
  (5 shorter events, 0.0 us)
Async XLA Ops:
  6.5 609.4 %all-gather.2.cloned.1.call-start = ((), (), s32[]{:S(2)}) async-start(), calls=%async_computation.2 | async-start | bytes 67092480 | tf_op jit(solution)/shard_map/all_gather | solution.py:56
  54.7 16.6 %copy-start = (bf16[1440,1536]{0,1:T(8,128)(2,1)S(1)}, bf16[1440,1536]{0,1:T(8,128)(2,1)}, u32[]{:S(2)}) copy-start(bf16[1440,1536]{0,1:T(8,128)(2,1)} %convert_element_type.30) | copy-start | bytes 13271044
  180.9 7.3 copy-start.1
  180.9 416.1 %all-to-all-start = ((bf16[91,384,256]{2,0,1:T(8,128)(2,1)}), bf16[91,384,256]{2,0,1:T(8,128)(2,1)}, u32[]{:S(2)}, u32[]{:S(2)}) async-start(bf16[91,384,256]{2,0,1:T(8,128)(2,1)} %copy.35), calls=%async_computation | async-start | bytes 37748736 | tf_op jit(solution)/shard_map/all_to_all | solution.py:45
Sparse Core Ops, SparseCore 0:
  8.9 320.7 all-gather.1
where the time goes:
time: 955 us; the launch traced here: 951 us
  waiting for transfers between devices  409 us (43%)
  blocking collectives  209 us (22%)
  local copies, waits for them, and re-layouts  174 us (18%)
  matrix products  85.8 us (9%)
  other arithmetic  52.6 us (6%)
  between operations  13.4 us (1%)
    all_to_all x1, waiting for transfers between devices, per_device(): lax.all_to_all(fourier.reshape(lat_rows, slot_count, 4 * chan_dev), 'lat'...  409 us
    all_to_all x1, blocking collectives, per_device(): lax.all_to_all(part_sums, 'ch', split_axis=0, concat_axis=3, tiled=True)  209 us
    dot_general x1, matrix products, per_device(): jnp.einsum('ack,kn->anc', masked, dft_basis, preferred_element_type=jnp.f...  49.8 us
    dot_general x1, local copies, waits for them, and re-layouts, project(): jnp.einsum('brl,lbn->brn', basis_piece, data_rows, preferred_element_type...  36 us
    dot_general x1, matrix products, project(): jnp.einsum('brl,lbn->brn', basis_piece, data_rows, preferred_element_type...  36 us
    all_to_all x2, local copies, waits for them, and re-layouts, per_device(): lax.all_to_all(part_sums, 'ch', split_axis=0, concat_axis=3, tiled=True)  34.7 us
    convert_element_type x1, local copies, waits for them, and re-layouts, per_device(): (fourier * norm_scale).astype(jnp.bfloat16)  31.3 us
    another operation x1, local copies, waits for them, and re-layouts, per_device(): fourier.reshape(lat_rows, slot_count, 4 * chan_dev)  28.4 us
  transfers between devices with their start and end apart: 2, of which 1 were waited for; matrix products, arithmetic and copies ran while one was open for 20% of the time, Pallas kernels for 0%

commit v1 on v0

--- a/solution.py
+++ b/solution.py
@@ -42,13 +42,11 @@
     dft_basis = dft_table(points, orders.reshape(-1), lon_count).reshape(lon_count, 4 * slot_count)
     fourier = jnp.einsum("ack,kn->anc", masked, dft_basis, preferred_element_type=jnp.float32)
     fourier = (fourier * norm_scale).astype(jnp.bfloat16).reshape(lat_rows, slot_count, 4, chan_dev)
-    received = lax.all_to_all(
-        fourier.reshape(lat_rows, slot_count, 4 * chan_dev),
-        "lat",
-        split_axis=1,
-        concat_axis=0,
-        tiled=True,
-    )
+    block = fourier.reshape(lat_rows, slot_count, 4 * chan_dev)
+    size = lax.axis_size("lat")
+    tiles = jnp.stack(jnp.split(block, size, axis=1), axis=0)
+    tiles = lax.all_to_all(tiles, "lat", split_axis=0, concat_axis=0)
+    received = jnp.concatenate(tiles, axis=0)
     group_start = lax.axis_index("lat") * group_size
     bound_group = lax.dynamic_slice_in_dim(bound_all, group_start, group_size)
     keep_group = lax.dynamic_slice_in_dim(keep_all, group_start, group_size)

time: 955 us -> 941 us (0.985)
  waiting for transfers between devices: 409 us -> 388 us
    unnamed x4 -> x13, local copies, waits for them, and re-layouts: 0.01 us -> 23.6 us
    all_to_all x1, waiting for transfers between devices: 409 us -> 387 us  [per_device(): tiles = lax.all_to_all(tiles, 'lat', split_axis=0, concat_axis=0)]
    all_to_all x1 -> x0, local copies, waits for them, and re-layouts: 19 us -> none  [per_device(): lax.all_to_all(fourier.reshape(lat_rows, slot_count, 4 * chan_dev), 'lat'...]
    another operation x1 -> x2, local copies, waits for them, and re-layouts: 28.4 us -> 31.9 us  [per_device(): tiles = jnp.stack(jnp.split(block, size, axis=1), axis=0)]
  transfers between devices with their start and end apart: 2 -> 2, of which waited for: 1 -> 1; matrix products, arithmetic and copies ran while one was open for 20% -> 21% of each run, Pallas kernels for 0% -> 0%
where the time goes in v1:
time: 941 us; the launch traced here: 937 us
  waiting for transfers between devices  388 us (41%)
  blocking collectives  209 us (22%)
  local copies, waits for them, and re-layouts  182 us (19%)
  matrix products  85.8 us (9%)
  other arithmetic  52.6 us (6%)
  between operations  13.4 us (1%)
    all_to_all x1, waiting for transfers between devices, per_device(): tiles = lax.all_to_all(tiles, 'lat', split_axis=0, concat_axis=0)  387 us
    all_to_all x1, blocking collectives, per_device(): lax.all_to_all(part_sums, 'ch', split_axis=0, concat_axis=3, tiled=True)  209 us
    dot_general x1, matrix products, per_device(): jnp.einsum('ack,kn->anc', masked, dft_basis, preferred_element_type=jnp.f...  49.8 us
    dot_general x1, local copies, waits for them, and re-layouts, project(): jnp.einsum('brl,lbn->brn', basis_piece, data_rows, preferred_element_type...  36 us
    dot_general x1, matrix products, project(): jnp.einsum('brl,lbn->brn', basis_piece, data_rows, preferred_element_type...  36 us
    all_to_all x2, local copies, waits for them, and re-layouts, per_device(): lax.all_to_all(part_sums, 'ch', split_axis=0, concat_axis=3, tiled=True)  34.7 us
    another operation x2, local copies, waits for them, and re-layouts, per_device(): tiles = jnp.stack(jnp.split(block, size, axis=1), axis=0)  31.9 us
    convert_element_type x1, local copies, waits for them, and re-layouts, per_device(): (fourier * norm_scale).astype(jnp.bfloat16)  31.3 us
  transfers between devices with their start and end apart: 2, of which 1 were waited for; matrix products, arithmetic and copies ran while one was open for 21% of the time, Pallas kernels for 0%

profile of v1, /device:TPU:0, one launch (start us, length us, event | category | flops | bytes accessed | tf_op | source)
XLA Modules:
  0.0 937.2 jit_solution(6972195727442938743)
XLA Ops:
  6.5 0.0 all-gather.2.cloned.1.call-start
  6.5 0.7 all-gather.2.cloned.1.call-update
  7.3 0.7 broadcast_subtract_fusion.1
  8.0 0.1 copy.34
  8.1 0.1 mul.66
  8.3 19.0 %cosine_convert_fusion = (bf16[1440,768,1]{1,0,2:T(8,128)(2,1)S(1)}, bf16[1440,768,1]{1,0,2:T(8,128)(2,1)S(1)}) fusion(s32[768]{0:T(1024)S(1)} %mul.66), kind=kLoop, calls=%fused_computation.18 | loop fusion | flops 13271040 | bytes 4426752 | tf_op jit(solution)/shard_map/convert
  27.3 3.2 pad_maximum_fusion
  30.6 13.2 %copy.35 = bf16[1440,768,2]{0,2,1:T(2,128)(2,1)} copy(bf16[1440,768,2]{1,0,2:T(8,128)(2,1)} %pad_maximum_fusion) | data formatting | bytes 8847360 | tf_op jit(solution)/shard_map/stack | solution.py:13
  43.8 10.9 %convert_element_type.30 = bf16[1440,1536]{0,1:T(8,128)(2,1)} reshape(bf16[1440,768,2]{0,2,1:T(2,128)(2,1)} %copy.35) | data formatting | bytes 8847360 | tf_op jit(solution)/shard_map/convert_element_type | solution.py:13
  54.7 0.0 copy-start.1
  54.7 16.6 %broadcast_select_fusion = bf16[91,64,1440]{2,1,0:T(8,128)(2,1)} fusion(bf16[91,64,1440]{2,1,0:T(8,128)(2,1)} %param.3, pred[91]{0:T(512)(128)(4,1)S(1)} %add_compare_fusion), kind=kLoop, calls=%fused_computation.10 | loop fusion | flops 8386560 | bytes 33546332 | tf_op jit(solution)/shard_map/jit(_where)/select_n | solution.py:39
  71.4 0.0 copy-done.1
  71.4 49.8 %fusion = bf16[91,1536,64]{1,0,2:T(8,128)(2,1)} fusion(bf16[91,64,1440]{2,1,0:T(8,128)(2,1)} %broadcast_select_fusion, bf16[1440,1536]{0,1:T(8,128)(2,1)S(1)} %copy-done.1), kind=kOutput, calls=%fused_computation.1 | convolution fusion | flops 25781403648 | bytes 39088128 | tf_op jit(solution)/shard_map/ack,kn->anc/dot_general | solution.py:43
  121.2 31.3 %copy.38 = bf16[91,1536,64]{0,2,1:T(8,128)(2,1)} copy(bf16[91,1536,64]{1,0,2:T(8,128)(2,1)} %fusion) | data formatting | bytes 35782656 | tf_op jit(solution)/shard_map/convert_element_type | solution.py:44
  152.5 0.0 copy-start
  152.5 4.2 fusion.25
  156.7 4.6 fusion.24
  161.3 4.7 fusion.23
  166.0 3.9 fusion.22
  169.9 0.0 copy-done
  169.9 2.0 fusion.21
  171.9 2.2 fusion.20
  174.1 2.0 fusion.19
  176.1 2.0 fusion.18
  178.1 29.9 %copy.39 = bf16[8,91,48,256]{3,2,1,0:T(8,128)(2,1)} copy(bf16[8,91,48,256]{1,3,2,0:T(8,128)(2,1)} %fusion.18) | data formatting | bytes 35782656 | tf_op jit(solution)/shard_map/stack | solution.py:47
  208.0 0.0 copy-start.2
  208.0 7.1 all-to-all-start
  215.1 0.1 dynamic_slice.6
  215.2 0.0 copy-done.2
  215.2 0.1 dynamic-slice_convert_fusion
  215.3 0.1 iota_compare_fusion
  215.4 386.8 %all-to-all-done = bf16[8,91,48,256]{3,2,1,0:T(8,128)(2,1)} async-done(((bf16[8,91,48,256]{3,2,1,0:T(8,128)(2,1)}), bf16[8,91,48,256]{3,2,1,0:T(8,128)(2,1)}, u32[]{:S(2)}, u32[]{:S(2)}) %all-to-all-start) | async-done | bytes 17891360 | tf_op jit(solution)/shard_map/all_to_all | solution.py:48
  602.2 0.0 all-gather.2.cloned.1.call-done
  602.2 36.0 %fusion.9 = f32[48,721,256]{2,1,0:T(8,128)} fusion(bf16[48,721,728]{2,1,0:T(8,128)(2,1)} %all-gather.2.cloned.1.call-done, bf16[728,48,256]{2,1,0:T(8,128)(2,1)} %bitcast.11), kind=kOutput, calls=%fused_computation.11 | convolution fusion | flops 12899647488 | bytes 103719168 | tf_op jit(solution)/shard_map/brl,lbn->brn/dot_general | solution.py:17
  638.2 36.0 %copy.41 = f32[48,721,256]{1,2,0:T(8,128)} copy(f32[48,721,256]{2,1,0:T(8,128)} %fusion.9) | data formatting | bytes 70877184 | tf_op jit(solution)/shard_map/brl,lbn->brn/dot_general | solution.py:17
  674.3 12.8 %fusion.2 = f32[48,721,2,64]{1,3,2,0:T(8,128)S(1)} fusion(f32[48,721,2,2,64]{1,4,3,2,0:T(8,128)} %bitcast.61, f32[48]{0:T(128)S(1)} %dynamic-slice_convert_fusion, pred[48,721]{1,0:T(8,128)(4,1)S(1)} %iota_compare_fusion), kind=kLoop, calls=%fused_computation.4 | loop fusion | flops 8859648 | bytes 53192688 | tf_op jit(solution)/shard_map/mul | solution.py:25
  687.1 208.6 %all_to_all.23 = f32[48,721,2,64]{1,3,2,0:T(8,128)S(1)} all-to-all(f32[48,721,2,64]{1,3,2,0:T(8,128)S(1)} %fusion.2), channel_id=1, replica_groups=mesh['lat'=8,'ch'=4] {'ch'}, dimensions={0} | all-to-all | bytes 35438592 | tf_op jit(solution)/shard_map/all_to_all | solution.py:56
  895.7 6.9 copy.43
  902.7 27.7 %copy.44 = f32[12,721,2,256]{3,2,1,0:T(2,128)} copy(f32[12,721,2,256]{1,3,2,0:T(8,128)} %bitcast.71) | data formatting | bytes 35438592 | tf_op jit(solution)/shard_map/all_to_all | solution.py:56
  (5 shorter events, 0.0 us)
Async XLA Ops:
  6.5 595.7 %all-gather.2.cloned.1.call-start = ((), (), s32[]{:S(2)}) async-start(), calls=%async_computation.2 | async-start | bytes 67092480 | tf_op jit(solution)/shard_map/all_gather | solution.py:54
  54.7 16.6 %copy-start.1 = (bf16[1440,1536]{0,1:T(8,128)(2,1)S(1)}, bf16[1440,1536]{0,1:T(8,128)(2,1)}, u32[]{:S(2)}) copy-start(bf16[1440,1536]{0,1:T(8,128)(2,1)} %convert_element_type.30) | copy-start | bytes 13271044
  152.5 17.4 %copy-start = (bf16[91,1536,64]{0,2,1:T(8,128)(2,1)S(1)}, bf16[91,1536,64]{0,2,1:T(8,128)(2,1)}, u32[]{:S(2)}) copy-start(bf16[91,1536,64]{0,2,1:T(8,128)(2,1)} %copy.38) | copy-start | bytes 53673988
  208.0 7.2 copy-start.2
  208.0 394.2 %all-to-all-start = ((bf16[8,91,48,256]{3,2,1,0:T(8,128)(2,1)}), bf16[8,91,48,256]{3,2,1,0:T(8,128)(2,1)}, u32[]{:S(2)}, u32[]{:S(2)}) async-start(bf16[8,91,48,256]{3,2,1,0:T(8,128)(2,1)} %copy.39), calls=%async_computation | async-start | bytes 35782656 | tf_op jit(solution)/shard_map/all_to_all | solution.py:48
Sparse Core Ops, SparseCore 0:
  8.9 320.7 all-gather.1
